TPU v7x, 256 devices: a 4x2x16 block of a 4x16x16 slice. The times are simulated.
256 devices in a mesh: groups: 2 (over y), mp: 16 (over z), expert: 4 (over x), dp: 2 (over core).
Axes of the slice: x: 4, y: 2, z: 16, core: 2. Of those that a mesh axis runs over, the one named last changes fastest.
The devices are a block of a 4x16x16 slice.
Arguments:
- hidden_in: bfloat16 [1024, 4096], P(('groups', 'expert', 'dp'), 'mp'), parts along dimension 0, may hold values from -6 to 6
- norm_gain: bfloat16 [2, 4096], P(None, 'mp'), may hold values from 0.25 to 1.75
- expert_ids: int32 [2, 1024, 2], P(None, ('groups', 'expert', 'dp')), parts along dimension 1, may hold values from 0 to 3, all different within a row; in each aligned block of 64 rows (0 to 63, 64 to 127, ..., all dimensions but the last counted through in order) at most 64 rows name the same one
- gate_counts: int32 [2, 1024, 2], P(None, ('groups', 'expert', 'dp')), parts along dimension 1, may hold values from 8 to 15
- exit_layer: int32 [1024], P(('groups', 'expert', 'dp')), parts along dimension 0, may hold values from 1 to 2
- w_gate: bfloat16 [2, 4, 7168, 4096], P(None, 'expert', ('mp', 'dp')), may hold values from -0.09375 to 0.09375
- w_up: bfloat16 [2, 4, 7168, 4096], P(None, 'expert', ('mp', 'dp')), may hold values from -0.09375 to 0.09375
- w_down: bfloat16 [2, 4, 7168, 4096], P(None, 'expert', ('mp', 'dp')), may hold values from -0.0625 to 0.0625
Outputs:
- hidden_out: bfloat16 [1024, 4096], P(('groups', 'expert', 'dp'), 'mp'), parts along dimension 0
There are 2 independent parts, one for each index of `groups`. A program takes and returns all parts, laid end to end along the dimension named above; an argument that names none is the same for every part. Nothing has to cross between parts.
Inputs may be any that keep to these rules, and one draw needn't show every extreme that they name: `expert_ids`: A token's two ids in a layer differ. In the rows of one device in one layer (aligned blocks of 64 rows, layer by layer) some expert may be named by all 64 rows.
All inputs are finite; a program needn't handle non-finite values.
Results may differ from a plain program's by a relative error of at most 0.014.
Values may be sent and summed in bfloat16 or wider, within the bound.
A program may use at most 128 MiB of HBM per device.

v0:
```python
import jax
import jax.numpy as jnp
from jax import lax
from jax.sharding import PartitionSpec as P

LAYERS = 2
norm_floor = 0.1


def rows_first(arrays, axis, dims):
    turned = [jnp.moveaxis(a, dim, 0) for a, dim in zip(arrays, dims)]
    both = jnp.concatenate([t.reshape(len(t), -1) for t in turned], axis=1)
    whole, at, outs = (lax.all_gather(both, axis, axis=0, tiled=True), 0, [])
    for t, dim in zip(turned, dims):
        section = whole[:, at : at + t[0].size].reshape(-1, *t.shape[1:])
        outs.append(jnp.moveaxis(section, 0, dim))
        at += t[0].size
    return tuple(outs)


def side_by_side(arrays, axis, dim, along):
    ends, at = ([], 0)
    for a in arrays[:-1]:
        at += a.shape[along]
        ends.append(at)
    both = jnp.concatenate(arrays, axis=along)
    return tuple(jnp.split(lax.all_gather(both, axis, axis=dim, tiled=True), ends, axis=along))


def body(hidden_in, norm_gain, expert_ids, gate_counts, exit_layer, w_gate, w_up, w_down):
    experts = lax.axis_size("expert")
    shards = lax.axis_size("mp")
    tok_rows, slice_width = hidden_in.shape
    full_width = slice_width * shards
    contract = (((1,), (1,)), ((), ()))
    expert_range = jnp.arange(experts, dtype=jnp.int32)
    slot_range = jnp.arange(tok_rows, dtype=jnp.int32)
    current = hidden_in
    for layer_idx in range(LAYERS):
        counts = gate_counts[layer_idx].astype(jnp.float32)
        gate_share = counts / jnp.sum(counts, axis=1, keepdims=True)
        active = exit_layer > layer_idx
        matched = (expert_ids[layer_idx][:, :, None] == expert_range[None, None, :]) & active[
            :, None, None
        ]
        chosen = jnp.sum(matched.astype(jnp.int32), axis=1)
        weight_te = jnp.sum(jnp.where(matched, gate_share[:, :, None], jnp.float32(0.0)), axis=1)
        slot_rank = jnp.cumsum(chosen, axis=0) - chosen
        place_mask = (slot_rank.T[:, None, :] == slot_range[None, :, None]) & (
            chosen.T[:, None, :] > 0
        )
        place_bf = place_mask.astype(jnp.bfloat16)
        current_f32 = current.astype(jnp.float32)
        whole_rows, whole_gain = rows_first((current, norm_gain[layer_idx]), "mp", (1, 0))
        whole_f32 = whole_rows.astype(jnp.float32)
        sum_squares = jnp.sum(whole_f32 * whole_f32, axis=1)
        inv_rms = lax.rsqrt(sum_squares / full_width + norm_floor)
        normed = (whole_f32 * inv_rms[:, None] * whole_gain.astype(jnp.float32)[None, :]).astype(
            jnp.bfloat16
        )
        outgoing = jnp.einsum(
            "ect,td->ecd", place_bf, normed, preferred_element_type=jnp.float32
        ).astype(jnp.bfloat16)
        incoming = lax.all_to_all(outgoing, "expert", split_axis=0, concat_axis=0, tiled=True)
        inputs = incoming.reshape(experts * tok_rows, full_width)
        gate_rows, up_rows, down_rows = side_by_side(
            (w_gate[layer_idx, 0], w_up[layer_idx, 0], w_down[layer_idx, 0]), "dp", 0, 1
        )
        gate_val = lax.dot_general(inputs, gate_rows, contract, preferred_element_type=jnp.float32)
        up_val = lax.dot_general(inputs, up_rows, contract, preferred_element_type=jnp.float32)
        hidden = (jax.nn.silu(gate_val) * up_val).astype(jnp.bfloat16)
        partial_value = jnp.dot(hidden, down_rows, preferred_element_type=jnp.float32)
        summed = lax.psum_scatter(
            partial_value.astype(jnp.bfloat16), "mp", scatter_dimension=1, tiled=True
        )
        returned = lax.all_to_all(
            summed.reshape(experts, tok_rows, slice_width),
            "expert",
            split_axis=0,
            concat_axis=0,
            tiled=True,
        )
        place_weight = place_mask.astype(jnp.float32) * weight_te.T[:, None, :]
        update = jnp.einsum("ect,ecd->td", place_weight, returned.astype(jnp.float32))
        current = (current_f32 + update).astype(jnp.bfloat16)
    return current


def solution(mesh):
    in_specs = (
        P(("groups", "expert", "dp"), "mp"),
        P(None, "mp"),
        P(None, ("groups", "expert", "dp"), None),
        P(None, ("groups", "expert", "dp"), None),
        P(("groups", "expert", "dp")),
        P(None, "expert", ("mp", "dp"), None),
        P(None, "expert", ("mp", "dp"), None),
        P(None, "expert", ("mp", "dp"), None),
    )
    out_specs = P(("groups", "expert", "dp"), "mp")
    return jax.shard_map(body, mesh=mesh, in_specs=in_specs, out_specs=out_specs, check_vma=False)
```

profile of v0, /device:TPU:40, one launch (start us, length us, event | category | flops | bytes accessed | tf_op | source)
XLA Modules:
  0.0 336.3 jit_solution(16841984590572916138)
XLA Ops:
  6.6 2.5 slice_bitcast_fusion.5
  9.1 0.6 copy-done
  9.7 1.1 copy-done.1
  10.8 2.8 slice_bitcast_fusion.3
  13.6 5.6 %pad_maximum_fusion = bf16[224,12288]{1,0:T(8,128)(2,1)} fusion(bf16[224,4096]{1,0:T(8,128)(2,1)S(1)} %get-tuple-element.11, bf16[224,4096]{1,0:T(8,128)(2,1)S(1)} %get-tuple-element.22, bf16[224,4096]{1,0:T(8,128)(2,1)S(1)} %get-tuple-element.7), kind=kLoop, calls=%fused_computation | loop fusion | flops 16515072 | bytes 11010048 | tf_op jit(solution)/shard_map/concatenate | solution.py:26
  19.3 0.5 copy-done.6
  19.8 0.1 copy.19
  20.2 51.8 %all_gather.12 = bf16[4096,65]{0,1:T(8,128)(2,1)S(1)} all-gather(bf16[256,65]{0,1:T(8,128)(2,1)S(1)} %pad_maximum_fusion.2), channel_id=1, replica_groups=mesh['groups'=2,'mp'=16,'expert'=4,'dp'=2] {'mp'}, dimensions={0}, use_global_device_ids=true | all-gather | bytes 565760 | tf_op jit(solution)/shard_map/all_gather | solution.py:13
  72.0 0.2 fusion.30
  72.2 0.9 convolution_convert_fusion.3
  73.1 23.9 %all_to_all.20 = bf16[4,64,4096]{2,1,0:T(8,128)(2,1)} all-to-all(bf16[4,64,4096]{2,1,0:T(8,128)(2,1)S(1)} %convolution_convert_fusion.3), channel_id=1, replica_groups=mesh['groups'=2,'mp'=16,'expert'=4,'dp'=2] {'expert'}, dimensions={0} | all-to-all | bytes 4194304 | tf_op jit(solution)/shard_map/all_to_all | solution.py:64
  97.0 3.8 %fusion.8 = f32[256,448]{0,1:T(8,128)S(1)} fusion(bf16[256,4096]{1,0:T(8,128)(2,1)} %bitcast.68, bf16[448,12288]{1,0:T(8,128)(2,1)} %all-gather.3.cloned.1.call-done), kind=kOutput, calls=%fused_computation.14 | convolution fusion | flops 939524096 | bytes 6225920 | tf_op jit(solution)/shard_map/dot_general | solution.py:69
  100.8 9.4 %convolution_convert_fusion.2 = bf16[256,4096]{1,0:T(8,128)(2,1)} fusion(bf16[448,12288]{1,0:T(8,128)(2,1)} %all-gather.3.cloned.1.call-done, bf16[256,4096]{1,0:T(8,128)(2,1)} %bitcast.69, f32[256,448]{0,1:T(8,128)S(1)} %fusion.8), kind=kOutput, calls=%fused_computation.4 | convolution fusion | flops 1880784896 | bytes 11993088 | tf_op jit(solution)/shard_map/dot_general | solution.py:72
  110.3 4.9 %pad_maximum_fusion.1 = bf16[224,12288]{1,0:T(8,128)(2,1)} fusion(bf16[224,4096]{1,0:T(8,128)(2,1)} %get-tuple-element.12, bf16[224,4096]{1,0:T(8,128)(2,1)} %get-tuple-element.21, bf16[224,4096]{1,0:T(8,128)(2,1)S(1)} %get-tuple-element.8), kind=kLoop, calls=%fused_computation.1 | loop fusion | flops 16515072 | bytes 11010048 | tf_op jit(solution)/shard_map/concatenate | solution.py:26
  115.3 0.1 copy.23
  115.6 0.3 copy-done.3
  115.9 57.0 %reduce-scatter.3.cloned.1.call-done = bf16[256,256]{1,0:T(8,128)(2,1)} async-done(((bf16[256,4096]{1,0:T(8,128)(2,1)}), bf16[256,256]{1,0:T(8,128)(2,1)}) %reduce-scatter.3.cloned.1.call-update) | async-done | bytes 131088 | tf_op jit(solution)/shard_map/reduce_scatter | solution.py:73
  172.9 4.3 %all-to-all-start.1 = ((bf16[4,64,256]{2,1,0:T(8,128)(2,1)}), bf16[4,64,256]{2,1,0:T(8,128)(2,1)S(1)}, u32[]{:S(2)}, u32[]{:S(2)}) async-start(bf16[4,64,256]{2,1,0:T(8,128)(2,1)} %bitcast.70), calls=%async_computation.2 | async-start | bytes 262144 | tf_op jit(solution)/shard_map/all_to_all | solution.py:76
  177.3 6.0 %all-to-all-done.1 = bf16[4,64,256]{2,1,0:T(8,128)(2,1)S(1)} async-done(((bf16[4,64,256]{2,1,0:T(8,128)(2,1)}), bf16[4,64,256]{2,1,0:T(8,128)(2,1)S(1)}, u32[]{:S(2)}, u32[]{:S(2)}) %all-to-all-start.1) | async-done | bytes 131104 | tf_op jit(solution)/shard_map/all_to_all | solution.py:76
  183.2 0.3 fusion.29
  183.5 30.7 %all_gather.14 = bf16[4096,65]{0,1:T(8,128)(2,1)S(1)} all-gather(bf16[256,65]{0,1:T(8,128)(2,1)S(1)} %pad_maximum_fusion.3), channel_id=1, replica_groups=mesh['groups'=2,'mp'=16,'expert'=4,'dp'=2] {'mp'}, dimensions={0}, use_global_device_ids=true | all-gather | bytes 565760 | tf_op jit(solution)/shard_map/all_gather | solution.py:13
  214.3 0.2 fusion.33
  214.5 2.2 convolution_convert_fusion.1
  216.7 3.7 %all-to-all-start.2 = ((bf16[4,64,4096]{2,1,0:T(8,128)(2,1)}), bf16[4,64,4096]{2,1,0:T(8,128)(2,1)S(1)}, u32[]{:S(2)}, u32[]{:S(2)}) async-start(bf16[4,64,4096]{2,1,0:T(8,128)(2,1)} %convolution_convert_fusion.1), calls=%async_computation.3 | async-start | bytes 4194304 | tf_op jit(solution)/shard_map/all_to_all | solution.py:64
  220.4 0.2 reduce-scatter.5.cloned.1.call-start
  220.7 16.1 %all-to-all-done.2 = bf16[4,64,4096]{2,1,0:T(8,128)(2,1)S(1)} async-done(((bf16[4,64,4096]{2,1,0:T(8,128)(2,1)}), bf16[4,64,4096]{2,1,0:T(8,128)(2,1)S(1)}, u32[]{:S(2)}, u32[]{:S(2)}) %all-to-all-start.2) | async-done | bytes 2097184 | tf_op jit(solution)/shard_map/all_to_all | solution.py:64
  236.8 3.2 fusion.3
  240.0 8.8 %convolution_convert_fusion = bf16[256,4096]{1,0:T(8,128)(2,1)} fusion(bf16[448,12288]{1,0:T(8,128)(2,1)} %all-gather.5.cloned.1.call-done, bf16[256,4096]{1,0:T(8,128)(2,1)S(1)} %bitcast.67, f32[256,448]{0,1:T(8,128)S(1)} %fusion.3), kind=kOutput, calls=%fused_computation.2 | convolution fusion | flops 1880784896 | bytes 11993088 | tf_op jit(solution)/shard_map/dot_general | solution.py:72
  248.9 69.8 %reduce-scatter.5.cloned.1.call-done = bf16[256,256]{1,0:T(8,128)(2,1)} async-done(((bf16[256,4096]{1,0:T(8,128)(2,1)}), bf16[256,256]{1,0:T(8,128)(2,1)}) %reduce-scatter.5.cloned.1.call-update) | async-done | bytes 131088 | tf_op jit(solution)/shard_map/reduce_scatter | solution.py:73
  318.7 4.2 %all-to-all-start.3 = ((bf16[4,64,256]{2,1,0:T(8,128)(2,1)}), bf16[4,64,256]{2,1,0:T(8,128)(2,1)S(1)}, u32[]{:S(2)}, u32[]{:S(2)}) async-start(bf16[4,64,256]{2,1,0:T(8,128)(2,1)} %bitcast.71), calls=%async_computation.5 | async-start | bytes 262144 | tf_op jit(solution)/shard_map/all_to_all | solution.py:76
  322.9 6.0 %all-to-all-done.3 = bf16[4,64,256]{2,1,0:T(8,128)(2,1)S(1)} async-done(((bf16[4,64,256]{2,1,0:T(8,128)(2,1)}), bf16[4,64,256]{2,1,0:T(8,128)(2,1)S(1)}, u32[]{:S(2)}, u32[]{:S(2)}) %all-to-all-start.3) | async-done | bytes 131104 | tf_op jit(solution)/shard_map/all_to_all | solution.py:76
  328.9 0.9 fusion.28
  (42 shorter events, 0.9 us)
Async XLA Ops:
  6.5 90.4 %all-gather.3.cloned.1.call-start = ((), (), s32[]{:S(2)}) async-start(), calls=%async_computation.6 | async-start | bytes 16515072 | tf_op jit(solution)/shard_map/all_gather | solution.py:27
  6.6 3.1 copy-start
  6.6 4.3 %copy-start.1 = (bf16[2,1,224,4096]{3,2,1,0:T(8,128)(2,1)S(1)}, bf16[2,1,224,4096]{3,2,1,0:T(8,128)(2,1)}, u32[]{:S(2)}) copy-start(bf16[2,1,224,4096]{3,2,1,0:T(8,128)(2,1)} %param.14) | copy-start | bytes 11010052
  19.1 0.7 copy-start.6
  19.1 0.7 copy-start.5
  19.1 1.0 copy-start.4
  19.1 1.0 copy-start.2
  19.2 153.7 %reduce-scatter.3.cloned.1.call-start = ((), (), s32[]{:S(2)}) async-start(), calls=%async_computation.7 | async-start | bytes 2228224 | tf_op jit(solution)/shard_map/reduce_scatter | solution.py:73
  110.2 110.5 %all-gather.5.cloned.1.call-start = ((), (), s32[]{:S(2)}) async-start(), calls=%async_computation.8 | async-start | bytes 16515072 | tf_op jit(solution)/shard_map/all_gather | solution.py:27
  115.2 0.7 copy-start.3
  172.9 10.3 %all-to-all-start.1 = ((bf16[4,64,256]{2,1,0:T(8,128)(2,1)}), bf16[4,64,256]{2,1,0:T(8,128)(2,1)S(1)}, u32[]{:S(2)}, u32[]{:S(2)}) async-start(bf16[4,64,256]{2,1,0:T(8,128)(2,1)} %bitcast.70), calls=%async_computation.2 | async-start | bytes 262144 | tf_op jit(solution)/shard_map/all_to_all | solution.py:76
  216.7 20.1 %all-to-all-start.2 = ((bf16[4,64,4096]{2,1,0:T(8,128)(2,1)}), bf16[4,64,4096]{2,1,0:T(8,128)(2,1)S(1)}, u32[]{:S(2)}, u32[]{:S(2)}) async-start(bf16[4,64,4096]{2,1,0:T(8,128)(2,1)} %convolution_convert_fusion.1), calls=%async_computation.3 | async-start | bytes 4194304 | tf_op jit(solution)/shard_map/all_to_all | solution.py:64
  220.4 98.3 %reduce-scatter.5.cloned.1.call-start = ((), (), s32[]{:S(2)}) async-start(), calls=%async_computation.9 | async-start | bytes 2228224 | tf_op jit(solution)/shard_map/reduce_scatter | solution.py:73
  318.7 10.2 %all-to-all-start.3 = ((bf16[4,64,256]{2,1,0:T(8,128)(2,1)}), bf16[4,64,256]{2,1,0:T(8,128)(2,1)S(1)}, u32[]{:S(2)}, u32[]{:S(2)}) async-start(bf16[4,64,256]{2,1,0:T(8,128)(2,1)} %bitcast.71), calls=%async_computation.5 | async-start | bytes 262144 | tf_op jit(solution)/shard_map/all_to_all | solution.py:76
Sparse Core Ops, SparseCore 0:
  19.3 45.2 all-gather.2
  110.4 62.5 reduce-scatter.2
  174.8 29.9 all-gather.4
  249.0 69.6 reduce-scatter.4
where the time goes:
time: 337 us; the launch traced here: 336 us
  waiting for transfers between devices  155 us (46%)
  blocking collectives  106 us (31%)
  matrix products  29.4 us (9%)
  between operations  13.3 us (4%)
  starting transfers between devices  12.6 us (4%)
  other arithmetic  11.3 us (3%)
  local copies, waits for them, and re-layouts  8.24 us (2%)
    reduce_scatter x2, waiting for transfers between devices, body(): lax.psum_scatter(partial_value.astype(jnp.bfloat16), 'mp', scatter_dimens...  127 us
    all_gather x2, blocking collectives, rows_first(): whole, at, outs = (lax.all_gather(both, axis, axis=0, tiled=True), 0, [])  82.5 us
    all_to_all x1, blocking collectives, body(): lax.all_to_all(outgoing, 'expert', split_axis=0, concat_axis=0, tiled=True)  23.9 us
    dot_general x2, matrix products, body(): jnp.dot(hidden, down_rows, preferred_element_type=jnp.float32)  18.2 us
    all_to_all x1, waiting for transfers between devices, body(): lax.all_to_all(outgoing, 'expert', split_axis=0, concat_axis=0, tiled=True)  16.1 us
    all_to_all x2, waiting for transfers between devices, body(): lax.all_to_all(summed.reshape(experts, tok_rows, slice_width), 'expert',...  11.9 us
    concatenate x2, other arithmetic, side_by_side(): both = jnp.concatenate(arrays, axis=along)  10.5 us
    all_to_all x2, starting transfers between devices, body(): lax.all_to_all(summed.reshape(experts, tok_rows, slice_width), 'expert',...  8.52 us
  transfers between devices with their start and end apart: 7, of which 5 were waited for; matrix products, arithmetic and copies ran while one was open for 3% of the time, Pallas kernels for 0%

commit v1 on v0

--- a/solution.py
+++ b/solution.py
@@ -5,6 +5,18 @@
 
 LAYERS = 2
 norm_floor = 0.1
+
+
+def cut_along(shard, dim, peers):
+    dims = shard.shape
+    tiles = shard.reshape(*dims[:dim], peers, dims[dim] // peers, *dims[dim + 1 :])
+    return jnp.moveaxis(tiles, dim, 0)
+
+
+def in_order(pieces, dim):
+    shape = list(pieces.shape[1:])
+    shape[dim] *= pieces.shape[0]
+    return jnp.moveaxis(pieces, 0, dim).reshape(shape)
 
 
 def rows_first(arrays, axis, dims):
@@ -61,7 +73,15 @@
         outgoing = jnp.einsum(
             "ect,td->ecd", place_bf, normed, preferred_element_type=jnp.float32
         ).astype(jnp.bfloat16)
-        incoming = lax.all_to_all(outgoing, "expert", split_axis=0, concat_axis=0, tiled=True)
+        size, mine = (lax.axis_size("expert"), lax.axis_index("expert"))
+        blocks = cut_along(outgoing, 0, size)
+        result = blocks
+        for step in range(1, size):
+            target, source = ((mine + step) % size, (mine - step) % size)
+            sent = lax.dynamic_index_in_dim(blocks, target, 0)
+            received = lax.ppermute(sent, "expert", [(i, (i + step) % size) for i in range(size)])
+            result = lax.dynamic_update_slice_in_dim(result, received, source, axis=0)
+        incoming = in_order(result, 0)
         inputs = incoming.reshape(experts * tok_rows, full_width)
         gate_rows, up_rows, down_rows = side_by_side(
             (w_gate[layer_idx, 0], w_up[layer_idx, 0], w_down[layer_idx, 0]), "dp", 0, 1

time: 337 us -> 342 us (1.015)
  blocking collectives: 106 us -> 82.5 us
  waiting for transfers between devices: 155 us -> 166 us
  local copies, waits for them, and re-layouts: 8.24 us -> 19.2 us
  starting transfers between devices: 12.6 us -> 18.4 us
    ppermute x0 -> x6, waiting for transfers between devices: none -> 25.4 us  [body(): lax.ppermute(sent, 'expert', [(i, (i + step) % size) for i in range(size)])]
    all_to_all x1 -> x0, blocking collectives: 23.9 us -> none  [body(): lax.all_to_all(outgoing, 'expert', split_axis=0, concat_axis=0, tiled=True)]
    all_to_all x1 -> x0, waiting for transfers between devices: 16.1 us -> none  [body(): lax.all_to_all(outgoing, 'expert', split_axis=0, concat_axis=0, tiled=True)]
    ppermute x0 -> x6, starting transfers between devices: none -> 9.6 us  [body(): lax.ppermute(sent, 'expert', [(i, (i + step) % size) for i in range(size)])]
    dynamic_update_slice x0 -> x6, local copies, waits for them, and re-layouts: none -> 8.14 us  [body(): result = lax.dynamic_update_slice_in_dim(result, received, source, axis=0)]
    all_to_all x1 -> x0, starting transfers between devices: 3.7 us -> none  [body(): lax.all_to_all(outgoing, 'expert', split_axis=0, concat_axis=0, tiled=True)]
  transfers between devices with their start and end apart: 7 -> 12, of which waited for: 5 -> 7; matrix products, arithmetic and copies ran while one was open for 3% -> 6% of each run, Pallas kernels for 0% -> 0%
where the time goes in v1:
time: 342 us; the launch traced here: 341 us
  waiting for transfers between devices  166 us (49%)
  blocking collectives  82.5 us (24%)
  matrix products  30.8 us (9%)
  local copies, waits for them, and re-layouts  19.2 us (6%)
  starting transfers between devices  18.4 us (5%)
  between operations  13.3 us (4%)
  other arithmetic  11.4 us (3%)
    reduce_scatter x2, waiting for transfers between devices, body(): lax.psum_scatter(partial_value.astype(jnp.bfloat16), 'mp', scatter_dimens...  128 us
    all_gather x2, blocking collectives, rows_first(): whole, at, outs = (lax.all_gather(both, axis, axis=0, tiled=True), 0, [])  82.5 us
    ppermute x6, waiting for transfers between devices, body(): lax.ppermute(sent, 'expert', [(i, (i + step) % size) for i in range(size)])  25.4 us
    dot_general x2, matrix products, body(): jnp.dot(hidden, down_rows, preferred_element_type=jnp.float32)  18.8 us
    all_to_all x2, waiting for transfers between devices, body(): lax.all_to_all(summed.reshape(experts, tok_rows, slice_width), 'expert',...  11.9 us
    concatenate x2, other arithmetic, side_by_side(): both = jnp.concatenate(arrays, axis=along)  10.6 us
    ppermute x6, starting transfers between devices, body(): lax.ppermute(sent, 'expert', [(i, (i + step) % size) for i in range(size)])  9.6 us
    all_to_all x2, starting transfers between devices, body(): lax.all_to_all(summed.reshape(experts, tok_rows, slice_width), 'expert',...  8.46 us
  transfers between devices with their start and end apart: 12, of which 7 were waited for; matrix products, arithmetic and copies ran while one was open for 6% of the time, Pallas kernels for 0%

profile of v1, /device:TPU:40, one launch (start us, length us, event | category | flops | bytes accessed | tf_op | source)
XLA Modules:
  0.0 341.3 jit_solution(5185642565627566390)
XLA Ops:
  6.6 2.6 slice_bitcast_fusion.5
  9.7 1.1 copy-done.2
  10.8 2.7 slice_bitcast_fusion.3
  13.5 5.5 %pad_maximum_fusion = bf16[224,12288]{1,0:T(8,128)(2,1)} fusion(bf16[224,4096]{1,0:T(8,128)(2,1)S(1)} %get-tuple-element.11, bf16[224,4096]{1,0:T(8,128)(2,1)S(1)} %get-tuple-element.28, bf16[224,4096]{1,0:T(8,128)(2,1)S(1)} %get-tuple-element.7), kind=kLoop, calls=%fused_computation | loop fusion | flops 16515072 | bytes 11010048 | tf_op jit(solution)/shard_map/concatenate | solution.py:38
  20.1 51.8 %all_gather.12 = bf16[4096,65]{0,1:T(8,128)(2,1)S(1)} all-gather(bf16[256,65]{0,1:T(8,128)(2,1)S(1)} %pad_maximum_fusion.2), channel_id=1, replica_groups=mesh['groups'=2,'mp'=16,'expert'=4,'dp'=2] {'mp'}, dimensions={0}, use_global_device_ids=true | all-gather | bytes 565760 | tf_op jit(solution)/shard_map/all_gather | solution.py:25
  72.1 0.9 convolution_convert_fusion.3
  73.0 1.3 copy-done
  74.4 1.7 collective-permute-start
  76.2 3.0 collective-permute-start.1
  79.2 1.3 collective-permute-start.2
  80.5 9.1 %collective-permute-done = bf16[1,1,64,4096]{3,2,0,1:T(8,128)(2,1)} collective-permute-done((bf16[1,1,64,4096]{3,2,0,1:T(8,128)(2,1)S(1)}, bf16[1,1,64,4096]{3,2,0,1:T(8,128)(2,1)}, u32[]{:S(2)}, u32[]{:S(2)}) %collective-permute-start) | collective-permute-done | bytes 524320 | tf_op jit(solution)/shard_map/ppermute | solution.py:82
  89.6 1.9 constant_dynamic-update-slice_fusion.5
  91.5 3.7 %collective-permute-done.1 = bf16[1,1,64,4096]{3,2,0,1:T(8,128)(2,1)} collective-permute-done((bf16[1,1,64,4096]{3,2,0,1:T(8,128)(2,1)S(1)}, bf16[1,1,64,4096]{3,2,0,1:T(8,128)(2,1)}, u32[]{:S(2)}, u32[]{:S(2)}) %collective-permute-start.1) | collective-permute-done | bytes 524320 | tf_op jit(solution)/shard_map/ppermute | solution.py:82
  95.2 1.9 constant_dynamic-update-slice_fusion.4
  97.1 1.9 constant_dynamic-update-slice_fusion.3
  99.0 3.8 %fusion.6 = f32[256,448]{0,1:T(8,128)S(1)} fusion(bf16[256,4096]{1,0:T(8,128)(2,1)} %bitcast.81, bf16[448,12288]{1,0:T(8,128)(2,1)} %all-gather.3.cloned.1.call-done), kind=kOutput, calls=%fused_computation.12 | convolution fusion | flops 939524096 | bytes 6225920 | tf_op jit(solution)/shard_map/dot_general | solution.py:90
  102.8 9.4 %convolution_convert_fusion.2 = bf16[256,4096]{1,0:T(8,128)(2,1)} fusion(bf16[448,12288]{1,0:T(8,128)(2,1)} %all-gather.3.cloned.1.call-done, f32[256,448]{0,1:T(8,128)S(1)} %fusion.6, bf16[256,4096]{1,0:T(8,128)(2,1)} %bitcast.82), kind=kOutput, calls=%fused_computation.4 | convolution fusion | flops 1880784896 | bytes 11993088 | tf_op jit(solution)/shard_map/dot_general | solution.py:92
  112.5 5.0 %pad_maximum_fusion.1 = bf16[224,12288]{1,0:T(8,128)(2,1)} fusion(bf16[224,4096]{1,0:T(8,128)(2,1)} %get-tuple-element.12, bf16[224,4096]{1,0:T(8,128)(2,1)} %get-tuple-element.27, bf16[224,4096]{1,0:T(8,128)(2,1)S(1)} %get-tuple-element.8), kind=kLoop, calls=%fused_computation.1 | loop fusion | flops 16515072 | bytes 11010048 | tf_op jit(solution)/shard_map/concatenate | solution.py:38
  118.3 58.2 %reduce-scatter.3.cloned.1.call-done = bf16[256,256]{1,0:T(8,128)(2,1)} async-done(((bf16[256,4096]{1,0:T(8,128)(2,1)}), bf16[256,256]{1,0:T(8,128)(2,1)}) %reduce-scatter.3.cloned.1.call-update) | async-done | bytes 131088 | tf_op jit(solution)/shard_map/reduce_scatter | solution.py:93
  176.5 4.3 %all-to-all-start = ((bf16[4,64,256]{2,1,0:T(8,128)(2,1)}), bf16[4,64,256]{2,1,0:T(8,128)(2,1)S(1)}, u32[]{:S(2)}, u32[]{:S(2)}) async-start(bf16[4,64,256]{2,1,0:T(8,128)(2,1)} %bitcast.83), calls=%async_computation.1 | async-start | bytes 262144 | tf_op jit(solution)/shard_map/all_to_all | solution.py:96
  180.8 6.0 %all-to-all-done = bf16[4,64,256]{2,1,0:T(8,128)(2,1)S(1)} async-done(((bf16[4,64,256]{2,1,0:T(8,128)(2,1)}), bf16[4,64,256]{2,1,0:T(8,128)(2,1)S(1)}, u32[]{:S(2)}, u32[]{:S(2)}) %all-to-all-start) | async-done | bytes 131104 | tf_op jit(solution)/shard_map/all_to_all | solution.py:96
  187.1 30.7 %all_gather.14 = bf16[4096,65]{0,1:T(8,128)(2,1)S(1)} all-gather(bf16[256,65]{0,1:T(8,128)(2,1)S(1)} %pad_maximum_fusion.3), channel_id=1, replica_groups=mesh['groups'=2,'mp'=16,'expert'=4,'dp'=2] {'mp'}, dimensions={0}, use_global_device_ids=true | all-gather | bytes 565760 | tf_op jit(solution)/shard_map/all_gather | solution.py:25
  218.0 2.2 convolution_convert_fusion.1
  220.2 1.5 dynamic-slice_bitcast_fusion
  222.4 2.1 collective-permute-start.4
  225.2 12.6 %collective-permute-done.3 = bf16[1,1,64,4096]{3,2,0,1:T(8,128)(2,1)S(1)} collective-permute-done((bf16[1,1,64,4096]{3,2,0,1:T(8,128)(2,1)S(1)}, bf16[1,1,64,4096]{3,2,0,1:T(8,128)(2,1)S(1)}, u32[]{:S(2)}, u32[]{:S(2)}) %collective-permute-start.3) | collective-permute-done | bytes 524320 | tf_op jit(solution)/shard_map/ppermute | solution.py:82
  240.3 3.9 %fusion.1 = f32[256,448]{0,1:T(8,128)S(1)} fusion(bf16[256,4096]{1,0:T(8,128)(2,1)} %bitcast.32, bf16[448,12288]{1,0:T(8,128)(2,1)} %all-gather.5.cloned.1.call-done), kind=kOutput, calls=%fused_computation.7 | convolution fusion | flops 939524096 | bytes 6225920 | tf_op jit(solution)/shard_map/dot_general | solution.py:90
  244.2 9.4 %convolution_convert_fusion = bf16[256,4096]{1,0:T(8,128)(2,1)} fusion(bf16[448,12288]{1,0:T(8,128)(2,1)} %all-gather.5.cloned.1.call-done, f32[256,448]{0,1:T(8,128)S(1)} %fusion.1, bf16[256,4096]{1,0:T(8,128)(2,1)} %bitcast.32), kind=kOutput, calls=%fused_computation.2 | convolution fusion | flops 1880784896 | bytes 11993088 | tf_op jit(solution)/shard_map/dot_general | solution.py:92
  253.6 70.0 %reduce-scatter.5.cloned.1.call-done = bf16[256,256]{1,0:T(8,128)(2,1)} async-done(((bf16[256,4096]{1,0:T(8,128)(2,1)}), bf16[256,256]{1,0:T(8,128)(2,1)}) %reduce-scatter.5.cloned.1.call-update) | async-done | bytes 131088 | tf_op jit(solution)/shard_map/reduce_scatter | solution.py:93
  323.6 4.2 %all-to-all-start.1 = ((bf16[4,64,256]{2,1,0:T(8,128)(2,1)}), bf16[4,64,256]{2,1,0:T(8,128)(2,1)S(1)}, u32[]{:S(2)}, u32[]{:S(2)}) async-start(bf16[4,64,256]{2,1,0:T(8,128)(2,1)} %bitcast.84), calls=%async_computation.3 | async-start | bytes 262144 | tf_op jit(solution)/shard_map/all_to_all | solution.py:96
  327.8 6.0 %all-to-all-done.1 = bf16[4,64,256]{2,1,0:T(8,128)(2,1)S(1)} async-done(((bf16[4,64,256]{2,1,0:T(8,128)(2,1)}), bf16[4,64,256]{2,1,0:T(8,128)(2,1)S(1)}, u32[]{:S(2)}, u32[]{:S(2)}) %all-to-all-start.1) | async-done | bytes 131104 | tf_op jit(solution)/shard_map/all_to_all | solution.py:96
  333.8 0.9 fusion.12
  (61 shorter events, 7.4 us)
Async XLA Ops:
  6.5 92.4 %all-gather.3.cloned.1.call-start = ((), (), s32[]{:S(2)}) async-start(), calls=%async_computation.4 | async-start | bytes 16515072 | tf_op jit(solution)/shard_map/all_gather | solution.py:39
  6.6 3.1 copy-start.1
  6.6 4.3 %copy-start.2 = (bf16[2,1,224,4096]{3,2,1,0:T(8,128)(2,1)S(1)}, bf16[2,1,224,4096]{3,2,1,0:T(8,128)(2,1)}, u32[]{:S(2)}) copy-start(bf16[2,1,224,4096]{3,2,1,0:T(8,128)(2,1)} %param.14) | copy-start | bytes 11010052
  19.0 0.7 copy-start.7
  19.0 0.7 copy-start.6
  19.1 1.0 copy-start.5
  19.1 1.0 copy-start.3
  19.1 157.4 %reduce-scatter.3.cloned.1.call-start = ((), (), s32[]{:S(2)}) async-start(), calls=%async_computation.5 | async-start | bytes 2228224 | tf_op jit(solution)/shard_map/reduce_scatter | solution.py:93
  73.0 1.3 copy-start
  74.4 15.2 %collective-permute-start = (bf16[1,1,64,4096]{3,2,0,1:T(8,128)(2,1)S(1)}, bf16[1,1,64,4096]{3,2,0,1:T(8,128)(2,1)}, u32[]{:S(2)}, u32[]{:S(2)}) collective-permute-start(bf16[1,1,64,4096]{3,2,0,1:T(8,128)(2,1)S(1)} %get-tuple-element.18), channel_id=1, source_target_pairs={{0,2},{2,4},{4,6},{6,0},{1,3},{3,5},{5,7},{7,1},{8,10},{10,12},{12... | collective-permute-start | bytes 1572872 | tf_op jit(solution)/shard_map/ppermute | solution.py:82
  76.2 19.1 %collective-permute-start.1 = (bf16[1,1,64,4096]{3,2,0,1:T(8,128)(2,1)S(1)}, bf16[1,1,64,4096]{3,2,0,1:T(8,128)(2,1)}, u32[]{:S(2)}, u32[]{:S(2)}) collective-permute-start(bf16[1,1,64,4096]{3,2,0,1:T(8,128)(2,1)S(1)} %get-tuple-element.17), channel_id=1, source_target_pairs={{0,4},{2,6},{4,0},{6,2},{1,5},{3,7},{5,1},{7,3},{8,12},{10,14},{12... | collective-permute-start | bytes 1572872 | tf_op jit(solution)/shard_map/ppermute | solution.py:82
  79.2 17.9 %collective-permute-start.2 = (bf16[1,1,64,4096]{3,2,0,1:T(8,128)(2,1)S(1)}, bf16[1,1,64,4096]{3,2,0,1:T(8,128)(2,1)}, u32[]{:S(2)}, u32[]{:S(2)}) collective-permute-start(bf16[1,1,64,4096]{3,2,0,1:T(8,128)(2,1)S(1)} %get-tuple-element.16), channel_id=1, source_target_pairs={{0,6},{2,0},{4,2},{6,4},{1,7},{3,1},{5,3},{7,5},{8,14},{10,8},{12,... | collective-permute-start | bytes 1572872 | tf_op jit(solution)/shard_map/ppermute | solution.py:82
  112.3 128.0 %all-gather.5.cloned.1.call-start = ((), (), s32[]{:S(2)}) async-start(), calls=%async_computation.6 | async-start | bytes 16515072 | tf_op jit(solution)/shard_map/all_gather | solution.py:39
  117.6 0.7 copy-start.4
  176.5 10.3 %all-to-all-start = ((bf16[4,64,256]{2,1,0:T(8,128)(2,1)}), bf16[4,64,256]{2,1,0:T(8,128)(2,1)S(1)}, u32[]{:S(2)}, u32[]{:S(2)}) async-start(bf16[4,64,256]{2,1,0:T(8,128)(2,1)} %bitcast.83), calls=%async_computation.1 | async-start | bytes 262144 | tf_op jit(solution)/shard_map/all_to_all | solution.py:96
  180.8 142.8 %reduce-scatter.5.cloned.1.call-start = ((), (), s32[]{:S(2)}) async-start(), calls=%async_computation.7 | async-start | bytes 2228224 | tf_op jit(solution)/shard_map/reduce_scatter | solution.py:93
  221.7 16.1 %collective-permute-start.3 = (bf16[1,1,64,4096]{3,2,0,1:T(8,128)(2,1)S(1)}, bf16[1,1,64,4096]{3,2,0,1:T(8,128)(2,1)S(1)}, u32[]{:S(2)}, u32[]{:S(2)}) collective-permute-start(bf16[1,1,64,4096]{3,2,0,1:T(8,128)(2,1)S(1)} %get-tuple-element.15), channel_id=1, source_target_pairs={{0,2},{2,4},{4,6},{6,0},{1,3},{3,5},{5,7},{7,1},{8,10},{10,12},{12... | collective-permute-start | bytes 1572872 | tf_op jit(solution)/shard_map/ppermute | solution.py:82
  222.4 16.3 %collective-permute-start.4 = (bf16[1,1,64,4096]{3,2,0,1:T(8,128)(2,1)S(1)}, bf16[1,1,64,4096]{3,2,0,1:T(8,128)(2,1)S(1)}, u32[]{:S(2)}, u32[]{:S(2)}) collective-permute-start(bf16[1,1,64,4096]{3,2,0,1:T(8,128)(2,1)S(1)} %get-tuple-element.14), channel_id=1, source_target_pairs={{0,4},{2,6},{4,0},{6,2},{1,5},{3,7},{5,1},{7,3},{8,12},{10,14},{12... | collective-permute-start | bytes 1572872 | tf_op jit(solution)/shard_map/ppermute | solution.py:82
  224.4 15.1 %collective-permute-start.5 = (bf16[1,1,64,4096]{3,2,0,1:T(8,128)(2,1)S(1)}, bf16[1,1,64,4096]{3,2,0,1:T(8,128)(2,1)S(1)}, u32[]{:S(2)}, u32[]{:S(2)}) collective-permute-start(bf16[1,1,64,4096]{3,2,0,1:T(8,128)(2,1)S(1)} %get-tuple-element.13), channel_id=1, source_target_pairs={{0,6},{2,0},{4,2},{6,4},{1,7},{3,1},{5,3},{7,5},{8,14},{10,8},{12,... | collective-permute-start | bytes 1572872 | tf_op jit(solution)/shard_map/ppermute | solution.py:82
  323.6 10.2 %all-to-all-start.1 = ((bf16[4,64,256]{2,1,0:T(8,128)(2,1)}), bf16[4,64,256]{2,1,0:T(8,128)(2,1)S(1)}, u32[]{:S(2)}, u32[]{:S(2)}) async-start(bf16[4,64,256]{2,1,0:T(8,128)(2,1)} %bitcast.84), calls=%async_computation.3 | async-start | bytes 262144 | tf_op jit(solution)/shard_map/all_to_all | solution.py:96
Sparse Core Ops, SparseCore 0:
  19.2 45.2 all-gather.2
  112.4 64.0 reduce-scatter.2
  178.4 29.6 all-gather.4
  253.7 69.8 reduce-scatter.4
